TPU v7x, 32 devices: a 4x4x1 block of a 4x4x8 slice. The times are simulated.
32 devices in a mesh: dp: 1 (over z), wg: 32 (over y, x, core).
Axes of the slice: x: 4, y: 4, z: 1, core: 2. Of those that a mesh axis runs over, the one named last changes fastest.
The devices are a block of a 4x4x8 slice.
Arguments:
- hidden: bfloat16 [65536, 1024], P(('dp', 'wg'))
- choice: int32 [65536, 8], P(('dp', 'wg'))
- pre_scale: float32 [1024], replicated
- w_router: bfloat16 [1024, 32], replicated
- w_gelu: bfloat16 [32, 1024, 512], P(None, None, 'wg')
- w_linear: bfloat16 [32, 1024, 512], P(None, None, 'wg')
- w_down: bfloat16 [32, 512, 1024], P(None, 'wg')
- post_scale: float32 [1024], replicated
Outputs:
- output: bfloat16 [65536, 1024], P(('dp', 'wg'))
All inputs are finite; a program needn't handle non-finite values.
Results may differ from a plain program's by a relative error of at most 0.001.
Values are sent between devices in bfloat16 or wider.
A program may use at most 768 MiB of HBM per device.

v0:
```python
import jax
import jax.numpy as jnp
from jax import lax
from jax.sharding import PartitionSpec as P

EPS = 1e-5


def rms_norm(values, gain_vec):
    return values * lax.rsqrt(jnp.mean(values * values, axis=-1, keepdims=True) + EPS) * gain_vec


def route_slots(block_ids, num_experts, capacity):
    tok_rows, top_k = block_ids.shape
    flat_ids = block_ids.reshape(-1)
    sort_order = jnp.argsort(flat_ids, stable=True)
    counts = jnp.sum((flat_ids[:, None] == jnp.arange(num_experts)[None, :]).astype(jnp.int32), axis=0)
    starts = jnp.cumsum(counts) - counts
    slot_rank = jnp.arange(capacity)
    source = jnp.minimum(starts[:, None] + slot_rank[None, :], tok_rows * top_k - 1)
    slot_token = sort_order[source].reshape(-1) // top_k
    sorted_pos = jnp.argsort(sort_order, stable=True)
    slot_of = flat_ids * capacity + sorted_pos - starts[flat_ids]
    return slot_token, slot_of


def solution(mesh):
    def local_block(hidden, choice, pre_scale, w_router, w_gelu, w_linear, w_down, post_scale):
        tok_rows, d_model = hidden.shape
        num_experts = w_gelu.shape[0]
        top_k = choice.shape[1]
        capacity = 2 * tok_rows * top_k // num_experts
        hidden_f = hidden.astype(jnp.float32)
        normed = rms_norm(hidden_f, pre_scale).astype(jnp.bfloat16)
        router_probs = jax.nn.softmax(jnp.dot(normed, w_router, preferred_element_type=jnp.float32), axis=-1)
        gate_vals = jnp.take_along_axis(router_probs, choice, axis=1)
        slot_token, slot_of = route_slots(choice, num_experts, capacity)
        dispatched = jnp.take(normed, slot_token, axis=0).reshape(num_experts, capacity, d_model)

        def one_expert(expert_args):
            expert_rows, gelu_part, linear_part, down_part = expert_args
            gelu_full = lax.all_gather(gelu_part, 'wg', axis=1, tiled=True)
            linear_full = lax.all_gather(linear_part, 'wg', axis=1, tiled=True)
            down_full = lax.all_gather(down_part, 'wg', axis=0, tiled=True)
            gelu_in = jnp.dot(expert_rows, gelu_full, preferred_element_type=jnp.float32)
            linear_in = jnp.dot(expert_rows, linear_full, preferred_element_type=jnp.float32)
            hidden_act = (jax.nn.gelu(gelu_in, approximate=True) * linear_in).astype(jnp.bfloat16)
            return jnp.dot(hidden_act, down_full, preferred_element_type=jnp.float32)

        expert_out = lax.map(one_expert, (dispatched, w_gelu, w_linear, w_down)).reshape(num_experts * capacity, d_model)
        picked = jnp.take(expert_out, slot_of, axis=0).reshape(tok_rows, top_k, d_model)
        mixed_out = jnp.sum(picked * gate_vals[:, :, None], axis=1)
        return (hidden_f + rms_norm(mixed_out, post_scale)).astype(jnp.bfloat16)

    row_spec = P(('dp', 'wg'), None)
    weight_in = P(None, None, 'wg')
    return jax.shard_map(local_block, mesh=mesh, in_specs=(row_spec, row_spec, P(), P(), weight_in, weight_in, P(None, 'wg', None), P()), out_specs=row_spec, check_vma=False)
```

profile of v0, /device:TPU:97, one launch (start us, length us, event | category | flops | bytes accessed | tf_op | source)
XLA Modules:
  0.0 4912.3 jit_solution(13598760204452495605)
XLA Ops:
  36.1 180.5 %gather_fusion = s32[32768]{0:T(1024)S(1)} fusion(s32[16384]{0:T(1024)S(1)} %get-tuple-element.39, s32[32768]{0:T(1024)S(1)} %broadcast_clamp_fusion.1), kind=kCustom, calls=%fused_computation | custom fusion | bytes 393216 | tf_op jit(solution)/shard_map/gather | solution.py:21
  246.6 130.6 %gather_fusion.3 = f32[16384]{0:T(1024)S(1)} fusion(f32[2048,32]{0,1:T(8,128)S(1)} %fusion.40, s32[16384]{0:T(1024)S(1)} %reshape.307), kind=kCustom, calls=%fused_computation.3 | custom fusion | bytes 262144 | tf_op jit(solution)/shard_map/jit(take_along_axis)/gather | solution.py:36
  379.4 161.9 %gather_fusion.1 = bf16[32768,1024]{1,0:T(8,128)(2,1)} fusion(bf16[2048,1024]{1,0:T(8,128)(2,1)} %copy-done.1, s32[32768]{0:T(1024)S(1)} %copy-done.6), kind=kCustom, calls=%fused_computation.1 | custom fusion | bytes 134348800 | tf_op jit(solution)/shard_map/jit(_take)/gather | solution.py:38
  541.3 44.3 broadcast_select_fusion
  585.6 3969.1 %while.10 = (s32[]{:T(128)}, f32[32,1024,1024]{2,1,0:T(8,128)}, bf16[32,1024,1024]{2,1,0:T(8,128)(2,1)}, bf16[32,1024,16]{1,2,0:T(8,128)(2,1)}, bf16[32,1024,16]...) while((s32[]{:T(128)}, f32[32,1024,1024]{2,1,0:T(8,128)}, bf16[32,1024,1024]{2,1,0:T(8,128)(2,1)}, ...), condition=%wide.region_6.7_spmd, body=%wide.region_5.6_spmd.sunk | while | flops 3226468352 | bytes 25658588 | solution.py:50
  590.4 40.1 all-gather.13.cloned.1.call-done
  669.3 38.8 all-gather.17.cloned.1.call-done
  793.0 38.7 all-gather.17.cloned.1.call-done
  917.0 38.8 all-gather.17.cloned.1.call-done
  1040.9 38.7 all-gather.17.cloned.1.call-done
  1288.2 38.7 all-gather.17.cloned.1.call-done
  1412.1 38.8 all-gather.17.cloned.1.call-done
  1536.3 38.7 all-gather.17.cloned.1.call-done
  1660.1 38.7 all-gather.17.cloned.1.call-done
  1784.2 38.7 all-gather.17.cloned.1.call-done
  2155.8 38.7 all-gather.17.cloned.1.call-done
  2279.9 38.8 all-gather.17.cloned.1.call-done
  2403.8 38.7 all-gather.17.cloned.1.call-done
  2650.9 38.7 all-gather.17.cloned.1.call-done
  2774.8 38.8 all-gather.17.cloned.1.call-done
  2898.9 38.8 all-gather.17.cloned.1.call-done
  3022.6 38.8 all-gather.17.cloned.1.call-done
  3270.5 38.7 all-gather.17.cloned.1.call-done
  3394.2 38.8 all-gather.17.cloned.1.call-done
  3518.0 38.7 all-gather.17.cloned.1.call-done
  3641.6 38.8 all-gather.17.cloned.1.call-done
  3765.4 38.8 all-gather.17.cloned.1.call-done
  3889.7 38.8 all-gather.17.cloned.1.call-done
  4013.5 38.7 all-gather.17.cloned.1.call-done
  4261.0 38.8 all-gather.17.cloned.1.call-done
  4509.1 38.8 all-gather.17.cloned.1.call-done
  4554.7 306.5 %gather_fusion.2 = f32[16384,1024]{1,0:T(8,128)} fusion(f32[32768,1024]{1,0:T(8,128)} %bitcast.42, s32[16384]{0:T(1024)S(1)} %copy-done.7), kind=kCustom, calls=%fused_computation.2 | custom fusion | bytes 134283264 | tf_op jit(solution)/shard_map/jit(_take)/gather | solution.py:51
  (488 shorter events, 3064.2 us)
Async XLA Ops:
  588.9 119.2 %all-gather.17.cloned.1.call-start = ((), (), s32[]{:S(2)}) async-start(), calls=%async_computation.2 | async-start | bytes 1081344 | tf_op jit(solution)/shard_map/while/body/eval_jaxpr/all_gather | solution.py:42
  717.9 113.7 %all-gather.17.cloned.1.call-start = ((), (), s32[]{:S(2)}) async-start(), calls=%async_computation.2 | async-start | bytes 1081344 | tf_op jit(solution)/shard_map/while/body/eval_jaxpr/all_gather | solution.py:42
  841.5 114.3 %all-gather.17.cloned.1.call-start = ((), (), s32[]{:S(2)}) async-start(), calls=%async_computation.2 | async-start | bytes 1081344 | tf_op jit(solution)/shard_map/while/body/eval_jaxpr/all_gather | solution.py:42
  965.7 113.9 %all-gather.17.cloned.1.call-start = ((), (), s32[]{:S(2)}) async-start(), calls=%async_computation.2 | async-start | bytes 1081344 | tf_op jit(solution)/shard_map/while/body/eval_jaxpr/all_gather | solution.py:42
  1089.4 114.0 %all-gather.17.cloned.1.call-start = ((), (), s32[]{:S(2)}) async-start(), calls=%async_computation.2 | async-start | bytes 1081344 | tf_op jit(solution)/shard_map/while/body/eval_jaxpr/all_gather | solution.py:42
  1213.2 113.7 %all-gather.17.cloned.1.call-start = ((), (), s32[]{:S(2)}) async-start(), calls=%async_computation.2 | async-start | bytes 1081344 | tf_op jit(solution)/shard_map/while/body/eval_jaxpr/all_gather | solution.py:42
  1336.7 114.2 %all-gather.17.cloned.1.call-start = ((), (), s32[]{:S(2)}) async-start(), calls=%async_computation.2 | async-start | bytes 1081344 | tf_op jit(solution)/shard_map/while/body/eval_jaxpr/all_gather | solution.py:42
  1460.8 114.2 %all-gather.17.cloned.1.call-start = ((), (), s32[]{:S(2)}) async-start(), calls=%async_computation.2 | async-start | bytes 1081344 | tf_op jit(solution)/shard_map/while/body/eval_jaxpr/all_gather | solution.py:42
  1584.8 114.0 %all-gather.17.cloned.1.call-start = ((), (), s32[]{:S(2)}) async-start(), calls=%async_computation.2 | async-start | bytes 1081344 | tf_op jit(solution)/shard_map/while/body/eval_jaxpr/all_gather | solution.py:42
  1708.7 114.2 %all-gather.17.cloned.1.call-start = ((), (), s32[]{:S(2)}) async-start(), calls=%async_computation.2 | async-start | bytes 1081344 | tf_op jit(solution)/shard_map/while/body/eval_jaxpr/all_gather | solution.py:42
  1832.7 114.2 %all-gather.17.cloned.1.call-start = ((), (), s32[]{:S(2)}) async-start(), calls=%async_computation.2 | async-start | bytes 1081344 | tf_op jit(solution)/shard_map/while/body/eval_jaxpr/all_gather | solution.py:42
  1956.7 114.2 %all-gather.17.cloned.1.call-start = ((), (), s32[]{:S(2)}) async-start(), calls=%async_computation.2 | async-start | bytes 1081344 | tf_op jit(solution)/shard_map/while/body/eval_jaxpr/all_gather | solution.py:42
  2080.7 113.9 %all-gather.17.cloned.1.call-start = ((), (), s32[]{:S(2)}) async-start(), calls=%async_computation.2 | async-start | bytes 1081344 | tf_op jit(solution)/shard_map/while/body/eval_jaxpr/all_gather | solution.py:42
  2204.4 114.3 %all-gather.17.cloned.1.call-start = ((), (), s32[]{:S(2)}) async-start(), calls=%async_computation.2 | async-start | bytes 1081344 | tf_op jit(solution)/shard_map/while/body/eval_jaxpr/all_gather | solution.py:42
  2328.6 113.9 %all-gather.17.cloned.1.call-start = ((), (), s32[]{:S(2)}) async-start(), calls=%async_computation.2 | async-start | bytes 1081344 | tf_op jit(solution)/shard_map/while/body/eval_jaxpr/all_gather | solution.py:42
  2452.2 113.7 %all-gather.17.cloned.1.call-start = ((), (), s32[]{:S(2)}) async-start(), calls=%async_computation.2 | async-start | bytes 1081344 | tf_op jit(solution)/shard_map/while/body/eval_jaxpr/all_gather | solution.py:42
  2575.7 113.9 %all-gather.17.cloned.1.call-start = ((), (), s32[]{:S(2)}) async-start(), calls=%async_computation.2 | async-start | bytes 1081344 | tf_op jit(solution)/shard_map/while/body/eval_jaxpr/all_gather | solution.py:42
  2699.4 114.2 %all-gather.17.cloned.1.call-start = ((), (), s32[]{:S(2)}) async-start(), calls=%async_computation.2 | async-start | bytes 1081344 | tf_op jit(solution)/shard_map/while/body/eval_jaxpr/all_gather | solution.py:42
  2823.4 114.3 %all-gather.17.cloned.1.call-start = ((), (), s32[]{:S(2)}) async-start(), calls=%async_computation.2 | async-start | bytes 1081344 | tf_op jit(solution)/shard_map/while/body/eval_jaxpr/all_gather | solution.py:42
  2947.6 113.9 %all-gather.17.cloned.1.call-start = ((), (), s32[]{:S(2)}) async-start(), calls=%async_computation.2 | async-start | bytes 1081344 | tf_op jit(solution)/shard_map/while/body/eval_jaxpr/all_gather | solution.py:42
  3071.3 114.2 %all-gather.17.cloned.1.call-start = ((), (), s32[]{:S(2)}) async-start(), calls=%async_computation.2 | async-start | bytes 1081344 | tf_op jit(solution)/shard_map/while/body/eval_jaxpr/all_gather | solution.py:42
  3195.3 113.9 %all-gather.17.cloned.1.call-start = ((), (), s32[]{:S(2)}) async-start(), calls=%async_computation.2 | async-start | bytes 1081344 | tf_op jit(solution)/shard_map/while/body/eval_jaxpr/all_gather | solution.py:42
  3319.0 114.0 %all-gather.17.cloned.1.call-start = ((), (), s32[]{:S(2)}) async-start(), calls=%async_computation.2 | async-start | bytes 1081344 | tf_op jit(solution)/shard_map/while/body/eval_jaxpr/all_gather | solution.py:42
  3442.8 113.9 %all-gather.17.cloned.1.call-start = ((), (), s32[]{:S(2)}) async-start(), calls=%async_computation.2 | async-start | bytes 1081344 | tf_op jit(solution)/shard_map/while/body/eval_jaxpr/all_gather | solution.py:42
  3566.6 113.9 %all-gather.17.cloned.1.call-start = ((), (), s32[]{:S(2)}) async-start(), calls=%async_computation.2 | async-start | bytes 1081344 | tf_op jit(solution)/shard_map/while/body/eval_jaxpr/all_gather | solution.py:42
  3690.2 114.0 %all-gather.17.cloned.1.call-start = ((), (), s32[]{:S(2)}) async-start(), calls=%async_computation.2 | async-start | bytes 1081344 | tf_op jit(solution)/shard_map/while/body/eval_jaxpr/all_gather | solution.py:42
  3814.2 114.3 %all-gather.17.cloned.1.call-start = ((), (), s32[]{:S(2)}) async-start(), calls=%async_computation.2 | async-start | bytes 1081344 | tf_op jit(solution)/shard_map/while/body/eval_jaxpr/all_gather | solution.py:42
  3938.3 113.9 %all-gather.17.cloned.1.call-start = ((), (), s32[]{:S(2)}) async-start(), calls=%async_computation.2 | async-start | bytes 1081344 | tf_op jit(solution)/shard_map/while/body/eval_jaxpr/all_gather | solution.py:42
  4062.0 114.0 %all-gather.17.cloned.1.call-start = ((), (), s32[]{:S(2)}) async-start(), calls=%async_computation.2 | async-start | bytes 1081344 | tf_op jit(solution)/shard_map/while/body/eval_jaxpr/all_gather | solution.py:42
  4185.8 114.0 %all-gather.17.cloned.1.call-start = ((), (), s32[]{:S(2)}) async-start(), calls=%async_computation.2 | async-start | bytes 1081344 | tf_op jit(solution)/shard_map/while/body/eval_jaxpr/all_gather | solution.py:42
  4309.7 114.0 %all-gather.17.cloned.1.call-start = ((), (), s32[]{:S(2)}) async-start(), calls=%async_computation.2 | async-start | bytes 1081344 | tf_op jit(solution)/shard_map/while/body/eval_jaxpr/all_gather | solution.py:42
  4433.6 114.3 %all-gather.17.cloned.1.call-start = ((), (), s32[]{:S(2)}) async-start(), calls=%async_computation.2 | async-start | bytes 1081344 | tf_op jit(solution)/shard_map/while/body/eval_jaxpr/all_gather | solution.py:42
  (75 other events, 9196.8 us)
Sparse Core Ops, SparseCore 0:
  588.8 41.6 all-gather.12
  671.4 36.6 all-gather.16
  717.6 36.7 all-gather.12
  919.1 36.6 all-gather.16
  965.3 36.7 all-gather.12
  1089.3 36.6 all-gather.12
  1212.8 36.6 all-gather.12
  1336.7 36.7 all-gather.12
  1460.7 36.6 all-gather.12
  1584.7 36.6 all-gather.12
  1832.6 36.6 all-gather.12
  1956.6 36.7 all-gather.12
  2080.3 36.7 all-gather.12
  2204.3 36.7 all-gather.12
  2328.2 36.7 all-gather.12
  2451.9 36.6 all-gather.12
  2575.4 36.7 all-gather.12
  2699.4 36.7 all-gather.12
  2823.4 36.7 all-gather.12
  2947.2 36.6 all-gather.12
  3071.2 36.7 all-gather.12
  3194.9 36.7 all-gather.12
  3318.6 36.7 all-gather.12
  3442.4 36.7 all-gather.12
  3566.2 36.6 all-gather.12
  3689.9 36.6 all-gather.12
  3814.1 36.6 all-gather.12
  3937.9 36.7 all-gather.12
  4061.9 36.7 all-gather.12
  4185.4 36.6 all-gather.12
  4309.7 36.7 all-gather.12
  4433.5 36.7 all-gather.12
  (64 shorter events, 2345.2 us)
where the time goes:
time: 4920 us; the launch traced here: 4910 us
  waiting for transfers between devices  3510 us (71%)
  local copies, waits for them, and re-layouts  922 us (19%)
  matrix products  322 us (7%)
  other arithmetic  139 us (3%)
    all_gather x32, waiting for transfers between devices, one_expert(): gelu_full = lax.all_gather(gelu_part, 'wg', axis=1, tiled=True)  1240 us
    all_gather x32, waiting for transfers between devices, one_expert(): down_full = lax.all_gather(down_part, 'wg', axis=0, tiled=True)  1140 us
    all_gather x32, waiting for transfers between devices, one_expert(): linear_full = lax.all_gather(linear_part, 'wg', axis=1, tiled=True)  1130 us
    gather x1, local copies, waits for them, and re-layouts, local_block(): jnp.take(expert_out, slot_of, axis=0).reshape(tok_rows, top_k, d_model)  306 us
    dot_general x32, matrix products, one_expert(): return jnp.dot(hidden_act, down_full, preferred_element_type=jnp.float32)  220 us
    gather x2, local copies, waits for them, and re-layouts, route_slots(): slot_token = sort_order[source].reshape(-1) // top_k  181 us
    gather x1, local copies, waits for them, and re-layouts, local_block(): jnp.take(normed, slot_token, axis=0).reshape(num_experts, capacity, d_model)  162 us
    gather x5, local copies, waits for them, and re-layouts, local_block(): gate_vals = jnp.take_along_axis(router_probs, choice, axis=1)  132 us
  transfers between devices with their start and end apart: 96, of which 96 were waited for; matrix products, arithmetic and copies ran while one was open for 4% of the time, Pallas kernels for 0%

commit v1 on v0

v1 whole, which is shorter than its diff:
```python
import jax
import jax.numpy as jnp
from jax import lax
from jax.sharding import PartitionSpec as P

EPS = 1e-5
CHUNKS = 4


def rms_norm(values, gain_vec):
    return values * lax.rsqrt(jnp.mean(values * values, axis=-1, keepdims=True) + EPS) * gain_vec


def solution(mesh):
    def local_block(hidden, choice, pre_scale, w_router, w_gelu, w_linear, w_down, post_scale):
        num_experts = w_gelu.shape[0]
        per = num_experts // CHUNKS
        gelu_t = jnp.swapaxes(w_gelu, 1, 2)
        linear_t = jnp.swapaxes(w_linear, 1, 2)
        own = jnp.stack([gelu_t, linear_t, w_down], axis=1)
        hidden_f = hidden.astype(jnp.float32)
        normed = rms_norm(hidden_f, pre_scale).astype(jnp.bfloat16)
        probs = jax.nn.softmax(jnp.dot(normed, w_router, preferred_element_type=jnp.float32), axis=-1)
        chosen = jnp.any(choice[:, :, None] == jnp.arange(num_experts)[None, None, :], axis=1)
        gates = jnp.where(chosen, probs, -1.0)

        total = jnp.zeros(hidden.shape, jnp.float32)
        for c in range(CHUNKS):
            full = lax.all_gather(own[c * per:(c + 1) * per], 'wg', axis=2, tiled=True)

            def one(i, acc):
                w = lax.dynamic_index_in_dim(full, i, 0, keepdims=False)
                dims = (((1,), (1,)), ((), ()))
                u = lax.dot_general(normed, w[0], dims, preferred_element_type=jnp.float32)
                v = lax.dot_general(normed, w[1], dims, preferred_element_type=jnp.float32)
                act = (jax.nn.gelu(u, approximate=True) * v).astype(jnp.bfloat16)
                out = jnp.dot(act, w[2], preferred_element_type=jnp.float32)
                g = lax.dynamic_slice_in_dim(gates, c * per + i, 1, 1)
                return acc + jnp.where(g >= 0, g * out, 0.0)

            total = lax.fori_loop(0, per, one, total)
        return (hidden_f + rms_norm(total, post_scale)).astype(jnp.bfloat16)

    row_spec = P(('dp', 'wg'), None)
    weight_in = P(None, None, 'wg')
    return jax.shard_map(local_block, mesh=mesh, in_specs=(row_spec, row_spec, P(), P(), weight_in, weight_in, P(None, 'wg', None), P()), out_specs=row_spec, check_vma=False)
```

time: 4920 us -> 721 us (0.15)
  waiting for transfers between devices: 3510 us -> 82.5 us
  local copies, waits for them, and re-layouts: 922 us -> 4.32 us
  matrix products: 322 us -> 601 us
  other arithmetic: 139 us -> 18.2 us
    all_gather x96 -> x4, waiting for transfers between devices: 3510 us -> 80.5 us  [local_block(): full = lax.all_gather(own[c * per:(c + 1) * per], 'wg', axis=2, tiled=True)]
    gather x11 -> x0, local copies, waits for them, and re-layouts: 783 us -> none  [the longest x1 306 us: local_block(): jnp.take(expert_out, slot_of, axis=0).reshape(tok_rows, top_k, d_model)]
    dot_general x64, matrix products: 320 us -> 600 us  [the longest x32 381 us: one(): out = jnp.dot(act, w[2], preferred_element_type=jnp.float32)]
    dynamic_slice x96 -> x0, local copies, waits for them, and re-layouts: 132 us -> none  [local_block(): lax.map(one_expert, (dispatched, w_gelu, w_linear, w_down))]
  transfers between devices with their start and end apart: 96 -> 4, of which waited for: 96 -> 1; matrix products, arithmetic and copies ran while one was open for 4% -> 63% of each run, Pallas kernels for 0% -> 0%
where the time goes in v1:
time: 721 us; the launch traced here: 720 us
  matrix products  601 us (83%)
  waiting for transfers between devices  82.5 us (11%)
  other arithmetic  18.2 us (3%)
  between operations  13.3 us (2%)
    dot_general x32, matrix products, one(): out = jnp.dot(act, w[2], preferred_element_type=jnp.float32)  381 us
    dot_general x32, matrix products, one(): u = lax.dot_general(normed, w[0], dims, preferred_element_type=jnp.float32)  219 us
    all_gather x4, waiting for transfers between devices, local_block(): full = lax.all_gather(own[c * per:(c + 1) * per], 'wg', axis=2, tiled=True)  80.5 us
  transfers between devices with their start and end apart: 4, of which 1 were waited for; matrix products, arithmetic and copies ran while one was open for 63% of the time, Pallas kernels for 0%

profile of v1, /device:TPU:97, one launch (start us, length us, event | category | flops | bytes accessed | tf_op | source)
XLA Modules:
  0.0 720.0 jit_solution(6681854415515539341)
XLA Ops:
  21.4 80.5 %all-gather.5.cloned.1.call-done = bf16[8,3,512,1024]{3,2,1,0:T(8,128)(2,1)} async-done(((bf16[8,3,16,1024]{3,2,1,0:T(8,128)(2,1)}), bf16[8,3,512,1024]{3,2,1,0:T(8,128)(2,1)}) %all-gather.5.cloned.1.call-update) | async-done | bytes 25165840 | tf_op jit(solution)/shard_map/all_gather | solution.py:29
  101.8 147.2 %while.62 = (s32[]{:T(128)}, f32[2048,1024]{1,0:T(8,128)}, f32[2048,32]{0,1:T(8,128)S(1)}, bf16[8,3,512,1024]{3,2,1,0:T(8,128)(2,1)}, bf16[2048,1024]{1,0:T(8,128)(2,1)}, /*index=5*/s32[]{:T(128)}, s32[]{:T(128)}, s32[]{}, s32[]{}) while((s32[]{:T(128)}, f32[2048,1024]{1,0:T(8,128)}, f32[2048,32]{0,1:T(8,128)S(1)}, ...), condition=%wide.region_5.6_spmd.clone, body=%wide.region_4.5_spmd.clone.sunk | while | flops 6461327360 | bytes 36730504 | solution.py:41
  126.1 11.7 %select_add_fusion.11 = f32[2048,1024]{1,0:T(8,128)} fusion(f32[2048,1024]{1,0:T(8,128)} %get-tuple-element.741, f32[2048]{0:T(1024)S(1)} %bitcast.164, pred[2048]{0:T(1024)(128)(4,1)S(1)} %get-tuple-element.730, pred[]{:T(512)S(6)} %compare.3, bf16[8,3,512,1024]{3,2,1,0:T(8,128)(2,1)} %get-tuple-element.752, s32[]{:T(128)} %get-tuple-element.740, ...), kind=kOutput, calls=%fused_computation.69.clone.1 | convolution fusion | flops 4313841664 | bytes 27274248 | tf_op jit(solution)/shard_map/while/body/eval_jaxpr/dot_general | solution.py:37
  144.6 11.7 %select_add_fusion.11 = f32[2048,1024]{1,0:T(8,128)} fusion(f32[2048,1024]{1,0:T(8,128)} %get-tuple-element.741, f32[2048]{0:T(1024)S(1)} %bitcast.164, pred[2048]{0:T(1024)(128)(4,1)S(1)} %get-tuple-element.730, pred[]{:T(512)S(6)} %compare.3, bf16[8,3,512,1024]{3,2,1,0:T(8,128)(2,1)} %get-tuple-element.752, s32[]{:T(128)} %get-tuple-element.740, ...), kind=kOutput, calls=%fused_computation.69.clone.1 | convolution fusion | flops 4313841664 | bytes 27274248 | tf_op jit(solution)/shard_map/while/body/eval_jaxpr/dot_general | solution.py:37
  200.3 11.7 %select_add_fusion.11 = f32[2048,1024]{1,0:T(8,128)} fusion(f32[2048,1024]{1,0:T(8,128)} %get-tuple-element.741, f32[2048]{0:T(1024)S(1)} %bitcast.164, pred[2048]{0:T(1024)(128)(4,1)S(1)} %get-tuple-element.730, pred[]{:T(512)S(6)} %compare.3, bf16[8,3,512,1024]{3,2,1,0:T(8,128)(2,1)} %get-tuple-element.752, s32[]{:T(128)} %get-tuple-element.740, ...), kind=kOutput, calls=%fused_computation.69.clone.1 | convolution fusion | flops 4313841664 | bytes 27274248 | tf_op jit(solution)/shard_map/while/body/eval_jaxpr/dot_general | solution.py:37
  249.1 151.3 %while.59 = (s32[]{:T(128)}, f32[2048,1024]{1,0:T(8,128)}, f32[2048,32]{0,1:T(8,128)S(1)}, bf16[8,3,512,1024]{3,2,1,0:T(8,128)(2,1)}, bf16[2048,1024]{1,0:T(8,12...) while((s32[]{:T(128)}, f32[2048,1024]{1,0:T(8,128)}, ...), condition=%wide.region_7.8_spmd, body=%wide.region_6.7_spmd.sunk | while | flops 6459230208 | bytes 36730560 | solution.py:41
  256.0 12.0 %select_add_fusion.8 = f32[2048,1024]{1,0:T(8,128)} fusion(f32[2048,1024]{1,0:T(8,128)} %get-tuple-element.770, f32[2048]{0:T(1024)S(1)} %bitcast.165, pred[2048]{0:T(1024)(128)(4,1)S(1)} %get-tuple-element.709, bf16[8,3,512,1024]{3,2,1,0:T(8,128)(2,1)} %get-tuple-element.783, s32[]{:T(128)} %get-tuple-element.769, s32[]{:T(128)S(6)} %add.488, ...), kind=kOutput, calls=%fused_computation.clone.1 | convolution fusion | flops 4311744512 | bytes 27274248 | tf_op jit(solution)/shard_map/while/body/eval_jaxpr/dot_general | solution.py:37
  274.9 12.0 %select_add_fusion.8 = f32[2048,1024]{1,0:T(8,128)} fusion(f32[2048,1024]{1,0:T(8,128)} %get-tuple-element.770, f32[2048]{0:T(1024)S(1)} %bitcast.165, pred[2048]{0:T(1024)(128)(4,1)S(1)} %get-tuple-element.709, bf16[8,3,512,1024]{3,2,1,0:T(8,128)(2,1)} %get-tuple-element.783, s32[]{:T(128)} %get-tuple-element.769, s32[]{:T(128)S(6)} %add.488, ...), kind=kOutput, calls=%fused_computation.clone.1 | convolution fusion | flops 4311744512 | bytes 27274248 | tf_op jit(solution)/shard_map/while/body/eval_jaxpr/dot_general | solution.py:37
  293.8 12.0 %select_add_fusion.8 = f32[2048,1024]{1,0:T(8,128)} fusion(f32[2048,1024]{1,0:T(8,128)} %get-tuple-element.770, f32[2048]{0:T(1024)S(1)} %bitcast.165, pred[2048]{0:T(1024)(128)(4,1)S(1)} %get-tuple-element.709, bf16[8,3,512,1024]{3,2,1,0:T(8,128)(2,1)} %get-tuple-element.783, s32[]{:T(128)} %get-tuple-element.769, s32[]{:T(128)S(6)} %add.488, ...), kind=kOutput, calls=%fused_computation.clone.1 | convolution fusion | flops 4311744512 | bytes 27274248 | tf_op jit(solution)/shard_map/while/body/eval_jaxpr/dot_general | solution.py:37
  312.7 12.0 %select_add_fusion.8 = f32[2048,1024]{1,0:T(8,128)} fusion(f32[2048,1024]{1,0:T(8,128)} %get-tuple-element.770, f32[2048]{0:T(1024)S(1)} %bitcast.165, pred[2048]{0:T(1024)(128)(4,1)S(1)} %get-tuple-element.709, bf16[8,3,512,1024]{3,2,1,0:T(8,128)(2,1)} %get-tuple-element.783, s32[]{:T(128)} %get-tuple-element.769, s32[]{:T(128)S(6)} %add.488, ...), kind=kOutput, calls=%fused_computation.clone.1 | convolution fusion | flops 4311744512 | bytes 27274248 | tf_op jit(solution)/shard_map/while/body/eval_jaxpr/dot_general | solution.py:37
  331.7 12.0 %select_add_fusion.8 = f32[2048,1024]{1,0:T(8,128)} fusion(f32[2048,1024]{1,0:T(8,128)} %get-tuple-element.770, f32[2048]{0:T(1024)S(1)} %bitcast.165, pred[2048]{0:T(1024)(128)(4,1)S(1)} %get-tuple-element.709, bf16[8,3,512,1024]{3,2,1,0:T(8,128)(2,1)} %get-tuple-element.783, s32[]{:T(128)} %get-tuple-element.769, s32[]{:T(128)S(6)} %add.488, ...), kind=kOutput, calls=%fused_computation.clone.1 | convolution fusion | flops 4311744512 | bytes 27274248 | tf_op jit(solution)/shard_map/while/body/eval_jaxpr/dot_general | solution.py:37
  350.6 12.0 %select_add_fusion.8 = f32[2048,1024]{1,0:T(8,128)} fusion(f32[2048,1024]{1,0:T(8,128)} %get-tuple-element.770, f32[2048]{0:T(1024)S(1)} %bitcast.165, pred[2048]{0:T(1024)(128)(4,1)S(1)} %get-tuple-element.709, bf16[8,3,512,1024]{3,2,1,0:T(8,128)(2,1)} %get-tuple-element.783, s32[]{:T(128)} %get-tuple-element.769, s32[]{:T(128)S(6)} %add.488, ...), kind=kOutput, calls=%fused_computation.clone.1 | convolution fusion | flops 4311744512 | bytes 27274248 | tf_op jit(solution)/shard_map/while/body/eval_jaxpr/dot_general | solution.py:37
  369.5 12.0 %select_add_fusion.8 = f32[2048,1024]{1,0:T(8,128)} fusion(f32[2048,1024]{1,0:T(8,128)} %get-tuple-element.770, f32[2048]{0:T(1024)S(1)} %bitcast.165, pred[2048]{0:T(1024)(128)(4,1)S(1)} %get-tuple-element.709, bf16[8,3,512,1024]{3,2,1,0:T(8,128)(2,1)} %get-tuple-element.783, s32[]{:T(128)} %get-tuple-element.769, s32[]{:T(128)S(6)} %add.488, ...), kind=kOutput, calls=%fused_computation.clone.1 | convolution fusion | flops 4311744512 | bytes 27274248 | tf_op jit(solution)/shard_map/while/body/eval_jaxpr/dot_general | solution.py:37
  388.4 12.0 %select_add_fusion.8 = f32[2048,1024]{1,0:T(8,128)} fusion(f32[2048,1024]{1,0:T(8,128)} %get-tuple-element.770, f32[2048]{0:T(1024)S(1)} %bitcast.165, pred[2048]{0:T(1024)(128)(4,1)S(1)} %get-tuple-element.709, bf16[8,3,512,1024]{3,2,1,0:T(8,128)(2,1)} %get-tuple-element.783, s32[]{:T(128)} %get-tuple-element.769, s32[]{:T(128)S(6)} %add.488, ...), kind=kOutput, calls=%fused_computation.clone.1 | convolution fusion | flops 4311744512 | bytes 27274248 | tf_op jit(solution)/shard_map/while/body/eval_jaxpr/dot_general | solution.py:37
  400.4 151.9 %while.60 = (s32[]{:T(128)}, f32[2048,1024]{1,0:T(8,128)}, f32[2048,32]{0,1:T(8,128)S(1)}, bf16[8,3,512,1024]{3,2,1,0:T(8,128)(2,1)}, bf16[2048,1024]{1,0:T(8,12...) while((s32[]{:T(128)}, f32[2048,1024]{1,0:T(8,128)}, ...), condition=%wide.region_9.10_spmd, body=%wide.region_8.9_spmd.sunk | while | flops 6459230208 | bytes 36730560 | solution.py:41
  407.4 12.0 %select_add_fusion.9 = f32[2048,1024]{1,0:T(8,128)} fusion(f32[2048,1024]{1,0:T(8,128)} %get-tuple-element.803, f32[2048]{0:T(1024)S(1)} %bitcast.166, pred[2048]{0:T(1024)(128)(4,1)S(1)} %get-tuple-element.716, bf16[8,3,512,1024]{3,2,1,0:T(8,128)(2,1)} %get-tuple-element.816, s32[]{:T(128)} %get-tuple-element.802, s32[]{:T(128)S(6)} %add.496, ...), kind=kOutput, calls=%fused_computation.23.clone.1 | convolution fusion | flops 4311744512 | bytes 27274248 | tf_op jit(solution)/shard_map/while/body/eval_jaxpr/dot_general | solution.py:37
  426.4 12.0 %select_add_fusion.9 = f32[2048,1024]{1,0:T(8,128)} fusion(f32[2048,1024]{1,0:T(8,128)} %get-tuple-element.803, f32[2048]{0:T(1024)S(1)} %bitcast.166, pred[2048]{0:T(1024)(128)(4,1)S(1)} %get-tuple-element.716, bf16[8,3,512,1024]{3,2,1,0:T(8,128)(2,1)} %get-tuple-element.816, s32[]{:T(128)} %get-tuple-element.802, s32[]{:T(128)S(6)} %add.496, ...), kind=kOutput, calls=%fused_computation.23.clone.1 | convolution fusion | flops 4311744512 | bytes 27274248 | tf_op jit(solution)/shard_map/while/body/eval_jaxpr/dot_general | solution.py:37
  445.3 12.0 %select_add_fusion.9 = f32[2048,1024]{1,0:T(8,128)} fusion(f32[2048,1024]{1,0:T(8,128)} %get-tuple-element.803, f32[2048]{0:T(1024)S(1)} %bitcast.166, pred[2048]{0:T(1024)(128)(4,1)S(1)} %get-tuple-element.716, bf16[8,3,512,1024]{3,2,1,0:T(8,128)(2,1)} %get-tuple-element.816, s32[]{:T(128)} %get-tuple-element.802, s32[]{:T(128)S(6)} %add.496, ...), kind=kOutput, calls=%fused_computation.23.clone.1 | convolution fusion | flops 4311744512 | bytes 27274248 | tf_op jit(solution)/shard_map/while/body/eval_jaxpr/dot_general | solution.py:37
  464.3 12.0 %select_add_fusion.9 = f32[2048,1024]{1,0:T(8,128)} fusion(f32[2048,1024]{1,0:T(8,128)} %get-tuple-element.803, f32[2048]{0:T(1024)S(1)} %bitcast.166, pred[2048]{0:T(1024)(128)(4,1)S(1)} %get-tuple-element.716, bf16[8,3,512,1024]{3,2,1,0:T(8,128)(2,1)} %get-tuple-element.816, s32[]{:T(128)} %get-tuple-element.802, s32[]{:T(128)S(6)} %add.496, ...), kind=kOutput, calls=%fused_computation.23.clone.1 | convolution fusion | flops 4311744512 | bytes 27274248 | tf_op jit(solution)/shard_map/while/body/eval_jaxpr/dot_general | solution.py:37
  483.3 12.0 %select_add_fusion.9 = f32[2048,1024]{1,0:T(8,128)} fusion(f32[2048,1024]{1,0:T(8,128)} %get-tuple-element.803, f32[2048]{0:T(1024)S(1)} %bitcast.166, pred[2048]{0:T(1024)(128)(4,1)S(1)} %get-tuple-element.716, bf16[8,3,512,1024]{3,2,1,0:T(8,128)(2,1)} %get-tuple-element.816, s32[]{:T(128)} %get-tuple-element.802, s32[]{:T(128)S(6)} %add.496, ...), kind=kOutput, calls=%fused_computation.23.clone.1 | convolution fusion | flops 4311744512 | bytes 27274248 | tf_op jit(solution)/shard_map/while/body/eval_jaxpr/dot_general | solution.py:37
  502.3 12.0 %select_add_fusion.9 = f32[2048,1024]{1,0:T(8,128)} fusion(f32[2048,1024]{1,0:T(8,128)} %get-tuple-element.803, f32[2048]{0:T(1024)S(1)} %bitcast.166, pred[2048]{0:T(1024)(128)(4,1)S(1)} %get-tuple-element.716, bf16[8,3,512,1024]{3,2,1,0:T(8,128)(2,1)} %get-tuple-element.816, s32[]{:T(128)} %get-tuple-element.802, s32[]{:T(128)S(6)} %add.496, ...), kind=kOutput, calls=%fused_computation.23.clone.1 | convolution fusion | flops 4311744512 | bytes 27274248 | tf_op jit(solution)/shard_map/while/body/eval_jaxpr/dot_general | solution.py:37
  521.3 12.0 %select_add_fusion.9 = f32[2048,1024]{1,0:T(8,128)} fusion(f32[2048,1024]{1,0:T(8,128)} %get-tuple-element.803, f32[2048]{0:T(1024)S(1)} %bitcast.166, pred[2048]{0:T(1024)(128)(4,1)S(1)} %get-tuple-element.716, bf16[8,3,512,1024]{3,2,1,0:T(8,128)(2,1)} %get-tuple-element.816, s32[]{:T(128)} %get-tuple-element.802, s32[]{:T(128)S(6)} %add.496, ...), kind=kOutput, calls=%fused_computation.23.clone.1 | convolution fusion | flops 4311744512 | bytes 27274248 | tf_op jit(solution)/shard_map/while/body/eval_jaxpr/dot_general | solution.py:37
  540.3 12.0 %select_add_fusion.9 = f32[2048,1024]{1,0:T(8,128)} fusion(f32[2048,1024]{1,0:T(8,128)} %get-tuple-element.803, f32[2048]{0:T(1024)S(1)} %bitcast.166, pred[2048]{0:T(1024)(128)(4,1)S(1)} %get-tuple-element.716, bf16[8,3,512,1024]{3,2,1,0:T(8,128)(2,1)} %get-tuple-element.816, s32[]{:T(128)} %get-tuple-element.802, s32[]{:T(128)S(6)} %add.496, ...), kind=kOutput, calls=%fused_computation.23.clone.1 | convolution fusion | flops 4311744512 | bytes 27274248 | tf_op jit(solution)/shard_map/while/body/eval_jaxpr/dot_general | solution.py:37
  552.3 151.1 %while.61 = (s32[]{:T(128)}, f32[2048,1024]{1,0:T(8,128)}, f32[2048,32]{0,1:T(8,128)S(1)}, bf16[8,3,512,1024]{3,2,1,0:T(8,128)(2,1)}, bf16[2048,1024]{1,0:T(8,12...) while((s32[]{:T(128)}, f32[2048,1024]{1,0:T(8,128)}, ...), condition=%wide.region_11.12_spmd, body=%wide.region_10.11_spmd.sunk | while | flops 6459230208 | bytes 36730560 | solution.py:41
  559.2 12.0 %select_add_fusion.10 = f32[2048,1024]{1,0:T(8,128)} fusion(f32[2048,1024]{1,0:T(8,128)} %get-tuple-element.836, f32[2048]{0:T(1024)S(1)} %bitcast.167, pred[2048]{0:T(1024)(128)(4,1)S(1)} %get-tuple-element.723, bf16[8,3,512,1024]{3,2,1,0:T(8,128)(2,1)} %get-tuple-element.849, s32[]{:T(128)} %get-tuple-element.835, s32[]{:T(128)S(6)} %add.504, ...), kind=kOutput, calls=%fused_computation.46.clone.1 | convolution fusion | flops 4311744512 | bytes 27274248 | tf_op jit(solution)/shard_map/while/body/eval_jaxpr/dot_general | solution.py:37
  578.0 12.0 %select_add_fusion.10 = f32[2048,1024]{1,0:T(8,128)} fusion(f32[2048,1024]{1,0:T(8,128)} %get-tuple-element.836, f32[2048]{0:T(1024)S(1)} %bitcast.167, pred[2048]{0:T(1024)(128)(4,1)S(1)} %get-tuple-element.723, bf16[8,3,512,1024]{3,2,1,0:T(8,128)(2,1)} %get-tuple-element.849, s32[]{:T(128)} %get-tuple-element.835, s32[]{:T(128)S(6)} %add.504, ...), kind=kOutput, calls=%fused_computation.46.clone.1 | convolution fusion | flops 4311744512 | bytes 27274248 | tf_op jit(solution)/shard_map/while/body/eval_jaxpr/dot_general | solution.py:37
  596.9 12.0 %select_add_fusion.10 = f32[2048,1024]{1,0:T(8,128)} fusion(f32[2048,1024]{1,0:T(8,128)} %get-tuple-element.836, f32[2048]{0:T(1024)S(1)} %bitcast.167, pred[2048]{0:T(1024)(128)(4,1)S(1)} %get-tuple-element.723, bf16[8,3,512,1024]{3,2,1,0:T(8,128)(2,1)} %get-tuple-element.849, s32[]{:T(128)} %get-tuple-element.835, s32[]{:T(128)S(6)} %add.504, ...), kind=kOutput, calls=%fused_computation.46.clone.1 | convolution fusion | flops 4311744512 | bytes 27274248 | tf_op jit(solution)/shard_map/while/body/eval_jaxpr/dot_general | solution.py:37
  615.8 12.0 %select_add_fusion.10 = f32[2048,1024]{1,0:T(8,128)} fusion(f32[2048,1024]{1,0:T(8,128)} %get-tuple-element.836, f32[2048]{0:T(1024)S(1)} %bitcast.167, pred[2048]{0:T(1024)(128)(4,1)S(1)} %get-tuple-element.723, bf16[8,3,512,1024]{3,2,1,0:T(8,128)(2,1)} %get-tuple-element.849, s32[]{:T(128)} %get-tuple-element.835, s32[]{:T(128)S(6)} %add.504, ...), kind=kOutput, calls=%fused_computation.46.clone.1 | convolution fusion | flops 4311744512 | bytes 27274248 | tf_op jit(solution)/shard_map/while/body/eval_jaxpr/dot_general | solution.py:37
  634.7 12.0 %select_add_fusion.10 = f32[2048,1024]{1,0:T(8,128)} fusion(f32[2048,1024]{1,0:T(8,128)} %get-tuple-element.836, f32[2048]{0:T(1024)S(1)} %bitcast.167, pred[2048]{0:T(1024)(128)(4,1)S(1)} %get-tuple-element.723, bf16[8,3,512,1024]{3,2,1,0:T(8,128)(2,1)} %get-tuple-element.849, s32[]{:T(128)} %get-tuple-element.835, s32[]{:T(128)S(6)} %add.504, ...), kind=kOutput, calls=%fused_computation.46.clone.1 | convolution fusion | flops 4311744512 | bytes 27274248 | tf_op jit(solution)/shard_map/while/body/eval_jaxpr/dot_general | solution.py:37
  653.6 12.0 %select_add_fusion.10 = f32[2048,1024]{1,0:T(8,128)} fusion(f32[2048,1024]{1,0:T(8,128)} %get-tuple-element.836, f32[2048]{0:T(1024)S(1)} %bitcast.167, pred[2048]{0:T(1024)(128)(4,1)S(1)} %get-tuple-element.723, bf16[8,3,512,1024]{3,2,1,0:T(8,128)(2,1)} %get-tuple-element.849, s32[]{:T(128)} %get-tuple-element.835, s32[]{:T(128)S(6)} %add.504, ...), kind=kOutput, calls=%fused_computation.46.clone.1 | convolution fusion | flops 4311744512 | bytes 27274248 | tf_op jit(solution)/shard_map/while/body/eval_jaxpr/dot_general | solution.py:37
  672.5 12.0 %select_add_fusion.10 = f32[2048,1024]{1,0:T(8,128)} fusion(f32[2048,1024]{1,0:T(8,128)} %get-tuple-element.836, f32[2048]{0:T(1024)S(1)} %bitcast.167, pred[2048]{0:T(1024)(128)(4,1)S(1)} %get-tuple-element.723, bf16[8,3,512,1024]{3,2,1,0:T(8,128)(2,1)} %get-tuple-element.849, s32[]{:T(128)} %get-tuple-element.835, s32[]{:T(128)S(6)} %add.504, ...), kind=kOutput, calls=%fused_computation.46.clone.1 | convolution fusion | flops 4311744512 | bytes 27274248 | tf_op jit(solution)/shard_map/while/body/eval_jaxpr/dot_general | solution.py:37
  691.4 12.0 %select_add_fusion.10 = f32[2048,1024]{1,0:T(8,128)} fusion(f32[2048,1024]{1,0:T(8,128)} %get-tuple-element.836, f32[2048]{0:T(1024)S(1)} %bitcast.167, pred[2048]{0:T(1024)(128)(4,1)S(1)} %get-tuple-element.723, bf16[8,3,512,1024]{3,2,1,0:T(8,128)(2,1)} %get-tuple-element.849, s32[]{:T(128)} %get-tuple-element.835, s32[]{:T(128)S(6)} %add.504, ...), kind=kOutput, calls=%fused_computation.46.clone.1 | convolution fusion | flops 4311744512 | bytes 27274248 | tf_op jit(solution)/shard_map/while/body/eval_jaxpr/dot_general | solution.py:37
  (109 shorter events, 302.8 us)
Async XLA Ops:
  6.5 13.3 %copy-start = (bf16[1024,32]{0,1:T(8,128)(2,1)S(1)}, bf16[1024,32]{0,1:T(8,128)(2,1)}, u32[]{:S(2)}) copy-start(bf16[1024,32]{0,1:T(8,128)(2,1)} %param.19) | copy-start | bytes 196612
  6.6 95.3 %all-gather.5.cloned.1.call-start = ((), (), s32[]{:S(2)}) async-start(), calls=%async_computation | async-start | bytes 25952256 | tf_op jit(solution)/shard_map/all_gather | solution.py:29
  10.7 5.6 copy-start.5
  10.7 5.9 copy-start.6
  10.7 238.4 %all-gather.7.cloned.1.call-start = ((), (), s32[]{:S(2)}) async-start(), calls=%async_computation.1 | async-start | bytes 25952256 | tf_op jit(solution)/shard_map/all_gather | solution.py:29
  11.5 388.9 %all-gather.9.cloned.1.call-start = ((), (), s32[]{:S(2)}) async-start(), calls=%async_computation.2 | async-start | bytes 25952256 | tf_op jit(solution)/shard_map/all_gather | solution.py:29
  12.3 539.9 %all-gather.11.cloned.1.call-start = ((), (), s32[]{:S(2)}) async-start(), calls=%async_computation.3 | async-start | bytes 25952256 | tf_op jit(solution)/shard_map/all_gather | solution.py:29
  13.0 3.6 copy-start.2
  17.9 2.0 copy-start.4
  703.4 4.6 copy-start.3
  703.4 4.6 copy-start.7
  708.0 5.5 copy-start.1
Sparse Core Ops, SparseCore 0:
  10.8 90.9 all-gather.4
  104.0 86.0 all-gather.6
  192.2 86.0 all-gather.8
  280.2 86.0 all-gather.10

commit v2 on v1

v2 whole, which is shorter than its diff:
```python
import functools

import jax
import jax.numpy as jnp
from jax import lax
from jax.experimental import pallas as pl
from jax.experimental.pallas import tpu as pltpu
from jax.sharding import PartitionSpec as P

EPS = 1e-5
MESH = pl.DeviceIdType.MESH
PARTS = 4
LAG = dict(G=1, F=2, D=6, C=14, B=21)
BURST = 5
NT = (((1,), (1,)), ((), ()))


def moe_kernel(side, hidden, choice_t, pre_scale, router_t, gelu_t, linear_t, down, post_scale,
               out, gathered, rows_in, normed, total, gates, weights, own, staged,
               load_sem, own_sem, slot_sem, out_sem, send_sem, recv_a, recv_b, recv_c, recv_d, recv_f):
    experts, width, d_model = down.shape
    unit = 3 * width
    plane = side * side
    tokens = rows_in.shape[0]
    part = tokens // PARTS
    me = lax.axis_index('wg')
    core = me % 2
    x = (me // 2) % side
    y = me // (2 * side)
    partner = me + 1 - 2 * core
    ramp = -(-max(LAG.values()) // PARTS)

    def ring(e):
        odd = e % 2
        a = x + odd * (y - x)
        b = y + odd * (x - y)
        a_step = 2 + odd * (2 * side - 2)
        b_step = 2 * side - odd * (2 * side - 2)
        base = me - a * a_step - b * b_step
        def at(i, j):
            return base + ((i + side) % side) * a_step + ((j + side) % side) * b_step
        return a, b, at

    def spot(i, j):
        return core * plane + ((j + side) % side) * side + (i + side) % side

    def push(src, dst, e, recv, device):
        pltpu.make_async_remote_copy(
            src_ref=src, dst_ref=dst, send_sem=send_sem.at[e], recv_sem=recv.at[e],
            device_id={'wg': device}, device_id_type=MESH).start()

    def settle(sem, e, units):
        ref = gathered.at[e, pl.ds(0, units)]
        pltpu.make_async_copy(ref, ref, sem).wait()

    def row(e, j, first=0, count=side):
        return gathered.at[e, pl.ds(core * plane + ((j + side) % side) * side + first, count)]

    def stage_a(e):
        a, b, at = ring(e)
        dst = gathered.at[e, spot(a, b)]
        push(own.at[e], dst, e, recv_a, at(a + 1, b))
        push(own.at[e], dst, e, recv_a, at(a - 1, b))

    def stage_b(e):
        a, b, at = ring(e)
        settle(recv_a.at[e], e, 2)
        low = gathered.at[e, spot(a - 1, b), pl.ds(0, unit // 2)]
        push(low, low, e, recv_b, at(a + 1, b))
        high = gathered.at[e, spot(a + 1, b), pl.ds(unit // 2, unit // 2)]
        push(high, high, e, recv_b, at(a - 1, b))

    def stage_c(e):
        a, b, at = ring(e)
        settle(recv_b.at[e], e, 1)
        mine = row(e, b)
        push(mine, mine, e, recv_c, at(a, b + 1))
        push(mine, mine, e, recv_c, at(a, b - 1))
        push(mine, mine, e, recv_f, partner)

    def stage_d(e):
        a, b, at = ring(e)
        settle(recv_c.at[e], e, 2 * side)
        low = row(e, b - 1, 0, side // 2)
        push(low, low, e, recv_d, at(a, b + 1))
        high = row(e, b + 1, side // 2, side // 2)
        push(high, high, e, recv_d, at(a, b - 1))
        for j in (b - 1, b + 1):
            whole = row(e, j)
            push(whole, whole, e, recv_f, partner)

    def stage_f(e):
        a, b, at = ring(e)
        settle(recv_d.at[e], e, side)
        whole = row(e, b + 2)
        push(whole, whole, e, recv_f, partner)

    def fetch(e):
        slot = e % 2
        return pltpu.make_async_copy(gathered.at[e], weights.at[slot], slot_sem.at[slot])

    def stage_g(e):
        settle(recv_f.at[e], e, plane)
        fetch(e).start()

    stages = dict(G=stage_g, F=stage_f, D=stage_d, C=stage_c, B=stage_b)

    def serve(step, k):
        for name, lag in LAG.items():
            if (k + lag) % PARTS == 0:
                e = step + (k + lag) // PARTS

                @pl.when(jnp.logical_and(e >= 0, e < experts))
                def _():
                    stages[name](e)
        if k == 0:
            ahead = step + ramp + BURST

            @pl.when(ahead < experts)
            def _():
                stage_a(ahead)

    def router(first, count):
        rows = pl.ds(first, count)
        h = rows_in[rows, :].astype(jnp.float32)
        scale = lax.rsqrt(jnp.mean(h * h, axis=-1, keepdims=True) + EPS)
        n = (h * scale * pre_scale[...]).astype(jnp.bfloat16)
        normed[rows, :] = n
        logits = lax.dot_general(router_t[...], n, NT, preferred_element_type=jnp.float32)
        top = jnp.max(logits, axis=0, keepdims=True)
        p = jnp.exp(logits - top)
        p = p / jnp.sum(p, axis=0, keepdims=True)
        names = lax.broadcasted_iota(jnp.int32, p.shape, 0)
        picks = choice_t[:, rows]
        hit = names == picks[0:1, :]
        for j in range(1, picks.shape[0]):
            hit = jnp.logical_or(hit, names == picks[j:j + 1, :])
        g = jnp.where(hit, p, -1.0)
        g = jnp.concatenate([g, jnp.full((128 - experts, count), -1.0, jnp.float32)], axis=0)
        gates[rows, :] = g.T

    def compute(e, k, last):
        slot = e % 2
        rows = pl.ds(k * part, part)
        n = normed[rows, :]
        wide = 2 * plane * width
        u = lax.dot_general(n, weights[slot, :, 0:width, :].reshape(wide, d_model), NT, preferred_element_type=jnp.float32)
        v = lax.dot_general(n, weights[slot, :, width:2 * width, :].reshape(wide, d_model), NT, preferred_element_type=jnp.float32)
        act = (jax.nn.gelu(u, approximate=True) * v).astype(jnp.bfloat16)
        o = jnp.dot(act, weights[slot, :, 2 * width:, :].reshape(wide, d_model), preferred_element_type=jnp.float32)
        lanes = lax.broadcasted_iota(jnp.int32, (part, 128), 1)
        g = jnp.sum(jnp.where(lanes == e, gates[rows, :], 0.0), axis=1, keepdims=True)
        total[rows, :] += jnp.where(g >= 0.0, g * o, 0.0)

    barrier = pltpu.get_barrier_semaphore()
    _, _, at0 = ring(0)
    friends = [at0(x + 1, y), at0(x - 1, y), at0(x, y + 1), at0(x, y - 1), partner]
    for device in friends:
        pl.semaphore_signal(barrier, inc=1, device_id={'wg': device}, device_id_type=MESH)
    loads = [pltpu.make_async_copy(src, own.at[:, pl.ds(i * width, width), :], own_sem)
             for i, src in enumerate((gelu_t, linear_t, down))]
    for copy in loads:
        copy.start()
    load_rows = pltpu.make_async_copy(hidden, rows_in, load_sem)
    load_rows.start()
    for copy in loads:
        copy.wait()
    pl.semaphore_wait(barrier, len(friends))

    def early(e, carry):
        stage_a(e)
        return carry
    lax.fori_loop(0, BURST, early, 0)

    def keep(e, carry):
        a, b, _ = ring(e)
        pltpu.make_async_copy(own.at[e], gathered.at[e, spot(a, b)], own_sem).start()
        return carry
    lax.fori_loop(0, experts, keep, 0)
    pltpu.make_async_copy(own, own, own_sem).wait()
    load_rows.wait()

    blocks = 4
    span = tokens // blocks

    def warm(r, carry):
        for k in range(PARTS):
            serve(r - ramp, k)
            if k == 0:
                @pl.when(r < blocks)
                def _():
                    def some(i, c):
                        router(pl.multiple_of(r * span + i * 256, 256), 256)
                        return c
                    lax.fori_loop(0, span // 256, some, 0)
                    total[pl.ds(r * span, span), :] = jnp.zeros((span, d_model), jnp.float32)
        return carry
    lax.fori_loop(0, ramp, warm, 0)

    def step(e, carry):
        for k in range(PARTS):
            serve(e, k)
            if k == 0:
                fetch(e).wait()
            compute(e, k, False)
        return carry
    lax.fori_loop(0, experts, step, 0)

    piece = staged.shape[1]
    def finish(i, carry):
        rows = pl.ds(pl.multiple_of(i * piece, piece), piece)
        t = total[rows, :]
        scale = lax.rsqrt(jnp.mean(t * t, axis=-1, keepdims=True) + EPS)
        slot = i % 2

        @pl.when(i >= 2)
        def _():
            pltpu.make_async_copy(staged.at[slot], out.at[rows, :], out_sem.at[slot]).wait()
        staged[slot] = (rows_in[rows, :].astype(jnp.float32) + t * scale * post_scale[...]).astype(jnp.bfloat16)
        pltpu.make_async_copy(staged.at[slot], out.at[rows, :], out_sem.at[slot]).start()
        return carry
    lax.fori_loop(0, tokens // piece, finish, 0)
    for slot in range(2):
        pltpu.make_async_copy(staged.at[slot], out.at[pl.ds(0, piece), :], out_sem.at[slot]).wait()

    def drain(e, carry):
        settle(send_sem.at[e], e, 2 * plane - 1)
        return carry
    lax.fori_loop(0, experts, drain, 0)


def solution(mesh):
    group = mesh.shape['wg']
    side = int(round((group // 2) ** 0.5))

    def local_block(hidden, choice, pre_scale, w_router, w_gelu, w_linear, w_down, post_scale):
        tokens, d_model = hidden.shape
        experts, width, _ = w_down.shape
        unit = 3 * width
        vmem = pl.BlockSpec(memory_space=pltpu.VMEM)
        hbm = pl.BlockSpec(memory_space=pl.ANY)
        flops = 6 * tokens * experts * group * width * d_model
        result, _ = pl.pallas_call(
            functools.partial(moe_kernel, side),
            out_shape=(jax.ShapeDtypeStruct((tokens, d_model), jnp.bfloat16),
                       jax.ShapeDtypeStruct((experts, group, unit, d_model), jnp.bfloat16)),
            in_specs=[hbm, vmem, vmem, vmem, hbm, hbm, hbm, vmem],
            out_specs=(hbm, hbm),
            scratch_shapes=[
                pltpu.VMEM((tokens, d_model), jnp.bfloat16),
                pltpu.VMEM((tokens, d_model), jnp.bfloat16),
                pltpu.VMEM((tokens, d_model), jnp.float32),
                pltpu.VMEM((tokens, 128), jnp.float32),
                pltpu.VMEM((2, group, unit, d_model), jnp.bfloat16),
                pltpu.VMEM((experts, unit, d_model), jnp.bfloat16),
                pltpu.VMEM((2, 256, d_model), jnp.bfloat16),
                pltpu.SemaphoreType.DMA,
                pltpu.SemaphoreType.DMA,
                pltpu.SemaphoreType.DMA((2,)),
                pltpu.SemaphoreType.DMA((2,)),
                pltpu.SemaphoreType.DMA((experts,)),
                pltpu.SemaphoreType.DMA((experts,)),
                pltpu.SemaphoreType.DMA((experts,)),
                pltpu.SemaphoreType.DMA((experts,)),
                pltpu.SemaphoreType.DMA((experts,)),
                pltpu.SemaphoreType.DMA((experts,)),
            ],
            compiler_params=pltpu.CompilerParams(
                collective_id=0, has_side_effects=True, vmem_limit_bytes=62 * 1024 * 1024),
            cost_estimate=pl.CostEstimate(flops=flops, bytes_accessed=4 * experts * group * unit * d_model, transcendentals=0),
            name='moe',
        )(hidden, choice.T, pre_scale.reshape(1, -1), w_router.T, jnp.swapaxes(w_gelu, 1, 2),
          jnp.swapaxes(w_linear, 1, 2), w_down, post_scale.reshape(1, -1))
        return result

    row_spec = P(('dp', 'wg'), None)
    weight_in = P(None, None, 'wg')
    return jax.shard_map(local_block, mesh=mesh, in_specs=(row_spec, row_spec, P(), P(), weight_in, weight_in, P(None, 'wg', None), P()), out_specs=row_spec, check_vma=False)
```

time: 721 us -> 301 us (0.42)
  matrix products: 601 us -> 0 us
  Pallas kernels: 0 us -> 295 us
  waiting for transfers between devices: 82.5 us -> 0 us
  other arithmetic: 18.2 us -> 0 us
  between operations: 13.3 us -> 0.01 us
    dot_general x65 -> x0, matrix products: 601 us -> none  [the longest x32 381 us: one(): out = jnp.dot(act, w[2], preferred_element_type=jnp.float32)]
    pallas_call x0 -> x1, Pallas kernels: none -> 295 us  [local_block(): pl.pallas_call(functools.partial(moe_kernel, side), out_shape=(jax.ShapeD...]
    all_gather x4 -> x0, waiting for transfers between devices: 80.5 us -> none  [local_block(): full = lax.all_gather(own[c * per:(c + 1) * per], 'wg', axis=2, tiled=True)]
    reduce_sum x3 -> x0, other arithmetic: 7.43 us -> none  [the longest x2 7.37 us: rms_norm(): jnp.mean(values * values, axis=-1, keepdims=True) + EPS]
  transfers between devices with their start and end apart: 4 -> 0, of which waited for: 1 -> 0; matrix products, arithmetic and copies ran while one was open for 63% -> 0% of each run, Pallas kernels for 0% -> 0%
where the time goes in v2:
time: 301 us; the launch traced here: 300 us
  Pallas kernels  295 us (98%)
  local copies, waits for them, and re-layouts  4.64 us (2%)
    pallas_call x1, Pallas kernels, local_block(): pl.pallas_call(functools.partial(moe_kernel, side), out_shape=(jax.ShapeD...  295 us

profile of v2, /device:TPU:97, one launch (start us, length us, event | category | flops | bytes accessed | tf_op | source)
XLA Modules:
  0.0 299.8 jit_solution(9953530614014221735)
XLA Ops:
  0.0 295.1 %moe.1 = (bf16[2048,1024]{1,0:T(8,128)(2,1)}, bf16[32,32,48,1024]{3,2,1,0:T(8,128)(2,1)}) custom-call(bf16[2048,1024]{1,0:T(8,128)(2,1)} %hidden.1, s32[8,2048]{1,0:T(8,128)} %bitcast.8, f32[1,1024]{1,0:T(1,128)} %bitcast.10, bf16[32,1024]{1,0:T(8,128)(2,1)} %bitcast.9, bf16[32,16,1024]{2,1,0:T(8,128)(2,1)} %bitcast.6, bf16[32,16,1024]{2,1,0:T(8,128)(2,1)} %bitcast.7, ...), custom_call_target="tpu_custom_call" | custom-call | flops 206158430208 | bytes 201326592 | tf_op jit(solution)/shard_map/moe/pallas_call | solution.py:243
  295.1 4.6 %copy.10 = bf16[2048,1024]{1,0:T(8,128)(2,1)} copy(bf16[2048,1024]{1,0:T(8,128)(2,1)} %get-tuple-element.6) | data formatting | bytes 8388608
